TPU v7x, 32 devices: a 4x2x2 block of a 4x4x8 slice. The times are simulated.
32 devices in a mesh: dp: 4 (over y, z), ep: 8 (over x, core).
Axes of the slice: x: 4, y: 2, z: 2, core: 2. Of those that a mesh axis runs over, the one named last changes fastest.
The devices are a block of a 4x4x8 slice.
Arguments:
- tokens: bfloat16 [4096, 2560], P(('dp', 'ep')), parts along dimension 0
- expert_ids: int32 [4096, 6], P(('dp', 'ep')), parts along dimension 0
- gate_vals: float32 [4096, 6], P(('dp', 'ep')), parts along dimension 0
- w_gate: bfloat16 [64, 2560, 1536], P('ep')
- w_up: bfloat16 [64, 2560, 1536], P('ep')
- w_down: bfloat16 [64, 1536, 2560], P('ep')
- shared_gate: bfloat16 [2560, 3072], replicated
- shared_up: bfloat16 [2560, 3072], replicated
- shared_down: bfloat16 [3072, 2560], replicated
Outputs:
- output: bfloat16 [4096, 2560], P(('dp', 'ep')), parts along dimension 0
There are 4 independent parts. A program takes and returns all parts, laid end to end along the dimension named above; an argument that names none is the same for every part.
All inputs are finite; a program needn't handle non-finite values.
Results may differ from a plain program's by a relative error of at most 0.00669141.
Values are sent between devices in bfloat16 or wider.
A program may use at most 768 MiB of HBM per device.

v0:
```python
import jax
import jax.numpy as jnp
from jax import lax
from jax.sharding import PartitionSpec as P


def swiglu(row_block, gate_w, up_w, down_w):
    gate_act = jnp.dot(row_block, gate_w, preferred_element_type=jnp.float32)
    up_act = jnp.dot(row_block, up_w, preferred_element_type=jnp.float32)
    hidden = (jax.nn.silu(gate_act) * up_act).astype(jnp.bfloat16)
    return jnp.dot(hidden, down_w, preferred_element_type=jnp.float32).astype(jnp.bfloat16)


def expert_block(recv_buf, w_gate, w_up, w_down):
    gate_act = jnp.einsum("slcd,ldf->slcf", recv_buf, w_gate, preferred_element_type=jnp.float32)
    up_act = jnp.einsum("slcd,ldf->slcf", recv_buf, w_up, preferred_element_type=jnp.float32)
    hidden = (jax.nn.silu(gate_act) * up_act).astype(jnp.bfloat16)
    return jnp.einsum("slcf,lfd->slcd", hidden, w_down, preferred_element_type=jnp.float32).astype(jnp.bfloat16)


def solution(mesh):
    group_size = mesh.shape["ep"]

    def moe_step(tokens, expert_ids, gate_vals, w_gate, w_up, w_down, shared_gate, shared_up, shared_down):
        tok_count, model_dim = tokens.shape
        top_count = expert_ids.shape[1]
        local_count = w_gate.shape[0]
        expert_count = local_count * group_size
        spread = max(group_size, expert_count // 2)
        capacity = (tok_count * top_count + spread - 1) // spread
        flat_ids = expert_ids.reshape(-1)
        one_hot = (flat_ids[:, None] == jnp.arange(expert_count, dtype=jnp.int32)[None, :]).astype(jnp.int32)
        slot_pos = jnp.sum(jnp.cumsum(one_hot, axis=0) * one_hot, axis=1) - 1
        columns = (flat_ids * capacity + slot_pos).reshape(tok_count, top_count)
        col_range = jnp.arange(expert_count * capacity, dtype=jnp.int32)
        dispatch = jnp.any(columns[:, :, None] == col_range[None, None, :], axis=1).astype(jnp.bfloat16)
        send_buf = jnp.einsum("tn,td->nd", dispatch, tokens, preferred_element_type=jnp.float32).astype(jnp.bfloat16)
        recv_buf = lax.all_to_all(send_buf, "ep", 0, 0, tiled=True)
        expert_out = expert_block(recv_buf.reshape(group_size, local_count, capacity, model_dim), w_gate, w_up, w_down)
        back_buf = lax.all_to_all(expert_out.reshape(expert_count * capacity, model_dim), "ep", 0, 0, tiled=True)
        picked = jnp.take(back_buf, columns, axis=0)
        shared_out = swiglu(tokens, shared_gate, shared_up, shared_down)
        result_acc = tokens.astype(jnp.float32) + jnp.sum(gate_vals[:, :, None] * picked.astype(jnp.float32), axis=1)
        return (result_acc + shared_out.astype(jnp.float32)).astype(jnp.bfloat16)

    row_spec = P(("dp", "ep"), None)
    expert_spec = P("ep", None, None)
    whole_spec = P(None, None)
    return jax.shard_map(moe_step, mesh=mesh, in_specs=(row_spec, row_spec, row_spec, expert_spec, expert_spec, expert_spec, whole_spec, whole_spec, whole_spec), out_specs=row_spec, check_vma=False)
```

profile of v0, /device:TPU:81, one launch (start us, length us, event | category | flops | bytes accessed | tf_op | source)
XLA Modules:
  0.0 326.4 jit_solution(14282740870870199098)
XLA Ops:
  0.0 0.8 copy.32
  0.8 0.1 eq.42
  0.9 0.1 eq.38
  1.1 1.8 reduce-window.6
  2.9 0.3 slice_reduce_fusion
  3.2 0.1 fusion.30
  3.4 0.1 sub.7
  3.5 0.1 copy.35
  3.5 1.2 compare_and_fusion
  4.8 0.0 copy-start.1
  4.8 0.6 copy-done.1
  5.4 0.8 fusion.24
  6.2 3.3 %convolution_convert_fusion = bf16[1536,2560]{1,0:T(8,128)(2,1)S(1)} fusion(pred[128,1536]{1,0:T(8,128)(4,1)S(1)} %fusion.24, bf16[128,2560]{1,0:T(8,128)(2,1)} %param.9), kind=kOutput, calls=%fused_computation.7 | convolution fusion | flops 1010565120 | bytes 8716288 | tf_op jit(solution)/shard_map/tn,td->nd/dot_general | solution.py:37
  9.5 93.8 %all_to_all.21 = bf16[8,192,2560]{2,1,0:T(8,128)(2,1)} all-to-all(bf16[8,192,2560]{2,1,0:T(8,128)(2,1)S(1)} %bitcast.79), channel_id=1, replica_groups=mesh['dp'=4,'ep'=8] {'ep'}, dimensions={0} | all-to-all | bytes 15728640 | tf_op jit(solution)/shard_map/all_to_all | solution.py:38
  103.3 27.9 %fusion.4 = f32[8,8,24,1536]{3,2,1,0:T(8,128)} fusion(bf16[8,2560,1536]{2,1,0:T(8,128)(2,1)} %param.12, bf16[8,8,24,2560]{3,2,1,0:T(8,128)(2,1)} %bitcast.77), kind=kOutput, calls=%fused_computation.5 | convolution fusion | flops 12079595520 | bytes 80216064 | tf_op jit(solution)/shard_map/slcd,ldf->slcf/dot_general | solution.py:15
  131.3 51.1 %convert_bitcast_fusion = bf16[8,8,24,2560]{3,2,0,1:T(8,128)(2,1)} fusion(bf16[8,1536,2560]{2,1,0:T(8,128)(2,1)} %param.14, f32[8,8,24,1536]{3,2,1,0:T(8,128)} %fusion.4, bf16[8,2560,1536]{2,1,0:T(8,128)(2,1)} %param.13, bf16[8,8,24,2560]{3,2,1,0:T(8,128)(2,1)} %bitcast.78), kind=kOutput, calls=%fused_computation.16 | convolution fusion | flops 24177278976 | bytes 150994944 | tf_op jit(solution)/shard_map/slcf,lfd->slcd/dot_general | solution.py:18
  182.3 7.1 %copy.39 = bf16[8,8,24,2560]{3,2,1,0:T(8,128)(2,1)} copy(bf16[8,8,24,2560]{3,2,0,1:T(8,128)(2,1)} %convert_bitcast_fusion) | data formatting | bytes 15728640 | tf_op jit(solution)/shard_map/convert_element_type | solution.py:18
  189.4 0.0 copy-start.2
  189.4 0.0 copy-start.4
  189.4 0.0 copy-start.3
  189.4 0.0 copy-start
  189.4 6.0 %all-to-all-start.1 = ((bf16[8,192,2560]{2,1,0:T(8,128)(2,1)}), bf16[8,192,2560]{2,1,0:T(8,128)(2,1)}, u32[]{:S(2)}, u32[]{:S(2)}) async-start(bf16[8,192,2560]{2,1,0:T(8,128)(2,1)} %bitcast.80), calls=%async_computation.1 | async-start | bytes 15728640 | tf_op jit(solution)/shard_map/all_to_all | solution.py:40
  195.5 0.0 copy-done.2
  195.5 0.1 copy.40
  195.6 0.1 reshape.49
  195.7 0.0 copy-done.4
  195.7 0.1 copy.36
  195.9 0.0 copy-done.3
  195.9 0.7 copy.31
  196.6 0.0 copy-done
  196.6 7.7 %fusion.34 = f32[128,3072]{1,0:T(8,128)S(1)} fusion(bf16[128,2560]{1,0:T(8,128)(2,1)S(1)} %copy-done, bf16[2560,3072]{1,0:T(8,128)(2,1)} %param.15), kind=kOutput, calls=%fused_computation.43 | convolution fusion | flops 2013265920 | bytes 17956864 | tf_op jit(solution)/shard_map/dot_general | solution.py:8
  204.3 79.1 %all-to-all-done.1 = bf16[8,192,2560]{2,1,0:T(8,128)(2,1)} async-done(((bf16[8,192,2560]{2,1,0:T(8,128)(2,1)}), bf16[8,192,2560]{2,1,0:T(8,128)(2,1)}, u32[]{:S(2)}, u32[]{:S(2)}) %all-to-all-start.1) | async-done | bytes 7864352 | tf_op jit(solution)/shard_map/all_to_all | solution.py:40
  283.4 12.6 %gather_fusion = bf16[768,2560]{1,0:T(8,128)(2,1)} fusion(bf16[1536,2560]{1,0:T(8,128)(2,1)} %bitcast.13, s32[1024]{0:T(1024)S(1)} %pad_clamp_fusion), kind=kCustom, calls=%fused_computation | custom fusion | bytes 7867392 | tf_op jit(solution)/shard_map/jit(_take)/gather | solution.py:41
  296.0 7.1 %reshape.48 = bf16[128,6,2560]{2,1,0:T(8,128)(2,1)} reshape(bf16[768,2560]{1,0:T(8,128)(2,1)} %gather_fusion) | data formatting | bytes 7864320 | tf_op jit(solution)/shard_map/jit(_take)/gather | solution.py:41
  303.2 8.1 %multiply_reduce_fusion = f32[128,2560]{1,0:T(8,128)S(1)} fusion(bf16[128,6,2560]{2,1,0:T(8,128)(2,1)} %reshape.48, f32[128,6]{1,0:T(8,128)} %copy.31, pred[128,6]{1,0:T(8,128)(4,1)S(1)} %copy.36), kind=kLoop, calls=%fused_computation.8 | loop fusion | flops 7536640 | bytes 5246720 | tf_op jit(solution)/shard_map/reduce_sum | solution.py:43
  311.3 15.1 %fusion.28 = bf16[128,2560]{1,0:T(8,128)(2,1)} fusion(bf16[3072,2560]{1,0:T(8,128)(2,1)} %param.17, f32[128,2560]{1,0:T(8,128)S(1)} %multiply_reduce_fusion, bf16[128,2560]{1,0:T(8,128)(2,1)S(1)} %copy-done, bf16[2560,3072]{1,0:T(8,128)(2,1)} %param.16, f32[128,3072]{1,0:T(8,128)S(1)} %fusion.34), kind=kOutput, calls=%fused_computation.27 | convolution fusion | flops 4030857216 | bytes 35651584 | tf_op jit(solution)/shard_map/dot_general | solution.py:11
  (5 shorter events, 0.1 us)
Async XLA Ops:
  4.8 0.6 copy-start.1
  189.4 6.0 %copy-start.2 = (s32[128,6]{0,1:T(8,128)S(1)}, s32[128,6]{0,1:T(8,128)}, u32[]{:S(2)}) copy-start(s32[128,6]{0,1:T(8,128)} %copy-done.1) | copy-start | bytes 9220
  189.4 6.3 %copy-start.4 = (pred[128,6]{0,1:T(8,128)(4,1)S(1)}, pred[128,6]{0,1:T(8,128)(4,1)}, u32[]{:S(2)}) copy-start(pred[128,6]{0,1:T(8,128)(4,1)} %get-tuple-element.5) | copy-start | bytes 2308
  189.4 6.5 %copy-start.3 = (f32[128,6]{0,1:T(8,128)S(1)}, f32[128,6]{0,1:T(8,128)}, u32[]{:S(2)}) copy-start(f32[128,6]{0,1:T(8,128)} %param.11) | copy-start | bytes 9220
  189.4 7.2 %copy-start = (bf16[128,2560]{1,0:T(8,128)(2,1)S(1)}, bf16[128,2560]{1,0:T(8,128)(2,1)}, u32[]{:S(2)}) copy-start(bf16[128,2560]{1,0:T(8,128)(2,1)} %param.9) | copy-start | bytes 1966084
  189.4 94.0 %all-to-all-start.1 = ((bf16[8,192,2560]{2,1,0:T(8,128)(2,1)}), bf16[8,192,2560]{2,1,0:T(8,128)(2,1)}, u32[]{:S(2)}, u32[]{:S(2)}) async-start(bf16[8,192,2560]{2,1,0:T(8,128)(2,1)} %bitcast.80), calls=%async_computation.1 | async-start | bytes 15728640 | tf_op jit(solution)/shard_map/all_to_all | solution.py:40
where the time goes:
time: 327 us; the launch traced here: 326 us
  matrix products  105 us (32%)
  blocking collectives  93.8 us (29%)
  waiting for transfers between devices  79.1 us (24%)
  local copies, waits for them, and re-layouts  30.1 us (9%)
  other arithmetic  12.1 us (4%)
  starting transfers between devices  6.04 us (2%)
    all_to_all x1, blocking collectives, moe_step(): recv_buf = lax.all_to_all(send_buf, 'ep', 0, 0, tiled=True)  93.8 us
    all_to_all x1, waiting for transfers between devices, moe_step(): lax.all_to_all(expert_out.reshape(expert_count * capacity, model_dim), 'e...  79.1 us
    dot_general x1, matrix products, expert_block(): jnp.einsum('slcf,lfd->slcd', hidden, w_down, preferred_element_type=jnp.f...  51.1 us
    dot_general x1, matrix products, expert_block(): jnp.einsum('slcd,ldf->slcf', recv_buf, w_gate, preferred_element_type=jnp...  27.9 us
    gather x2, local copies, waits for them, and re-layouts, moe_step(): picked = jnp.take(back_buf, columns, axis=0)  19.7 us
    dot_general x1, matrix products, swiglu(): jnp.dot(hidden, down_w, preferred_element_type=jnp.float32)  15.1 us
    reduce_sum x1, other arithmetic, moe_step(): jnp.sum(gate_vals[:, :, None] * picked.astype(jnp.float32), axis=1)  8.11 us
    dot_general x1, matrix products, swiglu(): gate_act = jnp.dot(row_block, gate_w, preferred_element_type=jnp.float32)  7.67 us
  transfers between devices with their start and end apart: 1, of which 1 were waited for; matrix products, arithmetic and copies ran while one was open for 3% of the time, Pallas kernels for 0%

commit v1 on v0

v1 whole, which is shorter than its diff:
```python
import functools

import jax
import jax.numpy as jnp
from jax import lax
from jax.experimental import pallas as pl
from jax.experimental.pallas import tpu as pltpu
from jax.sharding import PartitionSpec as P

F32 = jnp.float32
BF16 = jnp.bfloat16
NS = 5
NC = 5


def moe_kernel(dims, ids_ref, gates_ref, tok, wg, wu, wd, sg, su, sd, out_ref,
               xall, xown, xg, acc, h, y, pst, dsum, hrecv, frecv, oh, gt, hs, sgacc, shr, posr, grecv, gsend, slots,
               slot_sem, loc_sem, g_ssem, g_rsem, a_ssem, a_rsem, d_ssem, d_rsem, h_ssem, h_rsem, f_ssem, f_rsem):
    ng, nq, T, D, F, SF, E, cap, top = dims
    W = D // NC
    TC = W // 2
    NT = D // TC
    R = 2 * cap
    M = nq * R
    HT = T // 2
    FJ = F // W
    SFJ = SF // W
    n1 = NC * E
    ntot = n1 + 2 * NT + 2 * SFJ + NC

    me = lax.axis_index("ep")
    q = me // 2
    k = lax.rem(me, 2)
    lq = lax.rem(q + nq - 1, nq)
    rq = lax.rem(q + 1, nq)
    oq = lax.rem(q + 2, nq)
    sib = 2 * q + 1 - k
    left = 2 * lq + k
    right = 2 * rq + k
    opp = 2 * oq + k

    def rc(src, dst, ssem, rsem, dev):
        return pltpu.make_async_remote_copy(src_ref=src, dst_ref=dst, send_sem=ssem, recv_sem=rsem,
                                            device_id={"ep": dev}, device_id_type=pl.DeviceIdType.MESH)

    def issue(n):
        sl = lax.rem(n, NS)
        sem = slot_sem.at[sl]

        @pl.when(n < n1)
        def _():
            c = n // E
            e = lax.rem(n, E)
            for j in range(FJ):
                pltpu.make_async_copy(wg.at[e, pl.ds(pl.multiple_of(c * W, W), W), pl.ds(j * W, W)],
                                      slots.at[sl, pl.ds(j * W, W), :], sem).start()
            for j in range(FJ):
                pltpu.make_async_copy(wu.at[e, pl.ds(pl.multiple_of(c * W, W), W), pl.ds(j * W, W)],
                                      slots.at[sl, pl.ds((FJ + j) * W, W), :], sem).start()

        m = n - n1
        last = n >= ntot - 2
        r = lax.rem(m, 4)
        ct = jnp.where(last, NT - 1, m // 4)
        half = jnp.where(last, n - (ntot - 2), r)

        @pl.when((n >= n1) & (n < ntot) & ((r < 2) | last))
        def _():
            for j in range(E // 2):
                pltpu.make_async_copy(wd.at[half * (E // 2) + j, :, pl.ds(pl.multiple_of(ct * TC, TC), TC)],
                                      slots.at[sl, pl.ds((j // 2) * F, F), pl.ds((j % 2) * TC, TC)], sem).start()

        s = 2 * (m // 4) + r - 2
        shared = (n >= n1) & (n < ntot - 2) & (r >= 2)
        fcol = pl.ds(pl.multiple_of((s // 2) * W, W), W)

        @pl.when(shared & (s < 2 * SFJ) & (lax.rem(s, 2) == 0))
        def _():
            pltpu.make_async_copy(sg.at[:, fcol], slots.at[sl, pl.ds(0, D), :], sem).start()

        @pl.when(shared & (s < 2 * SFJ) & (lax.rem(s, 2) == 1))
        def _():
            pltpu.make_async_copy(su.at[:, fcol], slots.at[sl, pl.ds(0, D), :], sem).start()

        @pl.when(shared & (s >= 2 * SFJ))
        def _():
            col = pl.ds(pl.multiple_of((s - 2 * SFJ) * W, W), W)
            pltpu.make_async_copy(sd.at[:, col], slots.at[sl], sem).start()

    def wait_full(sl):
        pltpu.make_async_copy(sd.at[:, pl.ds(0, W)], slots.at[sl], slot_sem.at[sl]).wait()

    def wait_gu(sl):
        pltpu.make_async_copy(sg.at[:, pl.ds(0, W)], slots.at[sl, pl.ds(0, D), :], slot_sem.at[sl]).wait()

    xcopies = [pltpu.make_async_copy(tok.at[:, pl.ds(c * W, W)], xall.at[c, me], loc_sem.at[c]) for c in range(NC)]
    xcopies.append(pltpu.make_async_copy(tok, xown, loc_sem.at[NC]))
    for cp in xcopies:
        cp.start()
    for n in range(NS):
        issue(jnp.int32(n))

    eiota = lax.broadcasted_iota(jnp.int32, (ng * E, T), 0)
    dense = jnp.zeros((ng * E, T), F32)
    for j in range(top):
        dense = dense + jnp.where(ids_ref[j:j + 1, :] == eiota, gates_ref[j:j + 1, :], 0.0)
    gsend[...] = dense.reshape(ng, E, T)

    bar = pltpu.get_barrier_semaphore()
    for i in range(1, ng):
        pl.semaphore_signal(bar, inc=1, device_id={"ep": lax.rem(me + i, ng)}, device_id_type=pl.DeviceIdType.MESH)
    pl.semaphore_wait(bar, ng - 1)

    lo, hi = pl.ds(0, HT), pl.ds(HT, HT)

    def ag(c, typ, dev, src_dev, rows, dst_dev=None):
        ref = xall.at[c, src_dev] if rows is None else xall.at[c, src_dev, rows, :]
        return rc(ref, ref, a_ssem.at[c, typ], a_rsem.at[c, typ], dev)

    def own(c):
        ag(c, 0, right, me, lo).start()
        ag(c, 2, left, me, hi).start()
        ag(c, 1, right, me, hi).start()
        ag(c, 3, left, me, lo).start()
        ag(c, 6, sib, me, None).start()

    def svc0(c):
        ag(c, 0, left, left, lo).wait_recv()
        ag(c, 4, right, left, lo).start()
        ag(c, 2, right, right, hi).wait_recv()
        ag(c, 5, left, right, hi).start()

        @pl.when(c + 1 < NC)
        def _():
            own(c + 1)

    def svc1(c):
        ag(c, 1, left, left, hi).wait_recv()
        ag(c, 7, sib, left, None).start()
        ag(c, 3, right, right, lo).wait_recv()
        ag(c, 8, sib, right, None).start()

    def svc2(c):
        ag(c, 4, left, opp, lo).wait_recv()
        ag(c, 5, right, opp, hi).wait_recv()
        ag(c, 9, sib, opp, None).start()

    def need(c):
        sl_, sr_, so_ = 2 * lq + 1 - k, 2 * rq + 1 - k, 2 * oq + 1 - k
        ag(c, 6, sib, sib, None).wait_recv()
        ag(c, 7, sib, sl_, None).wait_recv()
        ag(c, 8, sib, sr_, None).wait_recv()
        ag(c, 9, sib, so_, None).wait_recv()

    for c in range(NC):
        xcopies[c].wait()
    own(jnp.int32(0))
    for i in range(1, ng):
        d = lax.rem(me + i, ng)
        rc(gsend.at[d], grecv.at[me], g_ssem.at[i], g_rsem.at[i], d).start()

    for e in range(E):
        acc[e] = jnp.zeros((M, 2 * F), F32)

    svc0(jnp.int32(0))

    for i in range(1, ng):
        s = lax.rem(me + ng - i, ng)
        rc(gsend.at[s], grecv.at[s], g_ssem.at[i], g_rsem.at[i], s).wait_recv()
    grecv[me] = gsend[me]
    gall = grecv[...].reshape(ng * E, T)
    mask = gall > 0.0
    tri = (lax.broadcasted_iota(jnp.int32, (T, T), 0) < lax.broadcasted_iota(jnp.int32, (T, T), 1)).astype(F32).astype(BF16)
    pos = jnp.dot(mask.astype(F32).astype(BF16), tri, preferred_element_type=F32)
    posr[...] = jnp.where(mask, pos, -1000.0).reshape(ng, E, T)

    svc1(jnp.int32(0))

    riota = lax.broadcasted_iota(jnp.int32, (R, T), 0).astype(F32)

    def route(b, _):
        parts = []
        for e in range(E):
            hits, gs = [], []
            for s in range(2):
                hit = posr[2 * b + s, e:e + 1, :] == (riota - float(s * cap))
                hits.append(jnp.where(hit, 1.0, 0.0))
                gs.append(jnp.where(hit, grecv[2 * b + s, e:e + 1, :], 0.0))
            oh[b, e] = jnp.concatenate(hits, axis=1).astype(BF16)
            parts.append(jnp.concatenate(gs, axis=1))
        g = jnp.concatenate(parts, axis=0).T
        g0 = g.astype(BF16)
        rem = g - g0.astype(F32)
        g1 = rem.astype(BF16)
        gt[b, 0] = g0
        gt[b, 1] = g1
        gt[b, 2] = (rem - g1.astype(F32)).astype(BF16)
        return 0

    lax.fori_loop(0, nq, route, 0)
    svc2(jnp.int32(0))

    def chunk(c, _):
        need(c)
        for b in range(nq):
            ohb = oh[b].reshape(E * R, 2 * T)
            xb = xall[c, 2 * b:2 * b + 2].reshape(2 * T, W)
            rows = jnp.dot(ohb, xb, preferred_element_type=F32).astype(BF16)
            xg[:, b * R:(b + 1) * R, :] = rows.reshape(E, R, W)

        def estep(e, _):
            n = c * E + e
            sl = lax.rem(n, NS)
            wait_full(sl)
            xe = xg[e]
            for j in range(2 * FJ):
                acc[e, :, j * W:(j + 1) * W] += jnp.dot(xe, slots[sl, j * W:(j + 1) * W, :], preferred_element_type=F32)
            issue(n + NS)

            @pl.when(c == NC - 1)
            def _():
                for j in range(FJ):
                    gv = acc[e, :, j * W:(j + 1) * W]
                    uv = acc[e, :, F + j * W:F + (j + 1) * W]
                    h[e, :, j * W:(j + 1) * W] = (gv * jax.nn.sigmoid(gv) * uv).astype(BF16)

            @pl.when((c < NC - 1) & (e == 1))
            def _():
                svc0(c + 1)

            @pl.when((c < NC - 1) & (e == 3))
            def _():
                svc1(c + 1)

            @pl.when((c < NC - 1) & (e == E - 2))
            def _():
                svc2(c + 1)
            return 0

        lax.fori_loop(0, E, estep, 0)
        return 0

    lax.fori_loop(0, NC, chunk, 0)

    def dcopy(ct, buf, dev):
        return rc(pst.at[buf, 1 - k], dsum.at[ct], d_ssem.at[ct], d_rsem.at[ct], dev)

    def hcopy(ct, i):
        rows = (lo, hi)[i]
        return rc(dsum.at[ct, oq, rows, :], hrecv.at[ct, i], h_ssem.at[ct, i], h_rsem.at[ct, i], (right, left)[i])

    def fcopy(ct, i):
        return rc(dsum.at[ct, (rq, lq)[i]], frecv.at[ct, i], f_ssem.at[ct, i], f_rsem.at[ct, i], (right, left)[i])

    def svca(ct):
        dcopy(ct, lax.rem(ct, 2), sib).wait_recv()
        for d in (oq, rq, lq, q):
            dsum[ct, d] += pst[lax.rem(ct, 2), k, d]
        hcopy(ct, 0).start()
        hcopy(ct, 1).start()

    def svcb(ct):
        hcopy(ct, 0).wait_recv()
        dsum[ct, rq, :HT, :] += hrecv[ct, 0]
        fcopy(ct, 0).start()
        hcopy(ct, 1).wait_recv()
        dsum[ct, lq, HT:, :] += hrecv[ct, 1]
        fcopy(ct, 1).start()

    def svcc(ct, _):
        fcopy(ct, 0).wait_recv()
        fcopy(ct, 1).wait_recv()
        cols = pl.ds(pl.multiple_of(ct * TC, TC), TC)
        routed = dsum[ct, q] + frecv[ct, 0] + frecv[ct, 1]
        out_ref[:, cols] = (xown[:, cols].astype(F32) + routed + shr[:, cols].astype(F32)).astype(BF16)
        return 0

    def shared_step(s, n):
        sl = lax.rem(n, NS)
        fcol = pl.ds(pl.multiple_of((s // 2) * W, W), W)

        @pl.when((s < 2 * SFJ) & (lax.rem(s, 2) == 0))
        def _():
            wait_gu(sl)
            sgacc[...] = jnp.dot(xown[...], slots[sl, :D, :], preferred_element_type=F32)

        @pl.when((s < 2 * SFJ) & (lax.rem(s, 2) == 1))
        def _():
            wait_gu(sl)
            uv = jnp.dot(xown[...], slots[sl, :D, :], preferred_element_type=F32)
            gv = sgacc[...]
            hs[:, fcol] = (gv * jax.nn.sigmoid(gv) * uv).astype(BF16)

        @pl.when(s >= 2 * SFJ)
        def _():
            wait_full(sl)
            col = pl.ds(pl.multiple_of((s - 2 * SFJ) * W, W), W)
            shr[:, col] = jnp.dot(hs[...], slots[sl], preferred_element_type=F32).astype(BF16)

        issue(n + NS)

    xcopies[NC].wait()

    def tile(ct, _):
        buf = lax.rem(ct, 2)
        base = n1 + 4 * ct - jnp.where(ct == NT - 1, 1, 0)

        def dstep(half, _):
            n = base + half
            sl = lax.rem(n, NS)
            wait_full(sl)
            for j in range(E // 2):
                e = half * (E // 2) + j
                w = slots[sl, (j // 2) * F:(j // 2 + 1) * F, (j % 2) * TC:(j % 2 + 1) * TC]
                ye = jnp.dot(h[e], w, preferred_element_type=F32).astype(BF16)
                y[:, e] = ye.reshape(nq, R, TC)
            issue(n + NS)
            return 0

        lax.fori_loop(0, 2, dstep, 0)

        @pl.when(ct >= 2)
        def _():
            dcopy(ct - 2, buf, sib).wait_send()

        def combine(b, _):
            yb = y[b].reshape(E * R, TC)
            p = jnp.dot(gt[b, 0], yb, preferred_element_type=F32)
            p = p + jnp.dot(gt[b, 1], yb, preferred_element_type=F32)
            p = p + jnp.dot(gt[b, 2], yb, preferred_element_type=F32)
            pst[buf, 0, b] = p[:T]
            pst[buf, 1, b] = p[T:]
            return 0

        lax.fori_loop(0, nq, combine, 0)
        dcopy(ct, buf, sib).start()

        @pl.when(ct < NT - 1)
        def _():
            shared_step(2 * ct, base + 2)

        svca(ct)

        @pl.when(ct >= 1)
        def _():
            svcb(ct - 1)

        @pl.when(ct < NT - 2)
        def _():
            shared_step(2 * ct + 1, base + 3)
        return 0

    lax.fori_loop(0, NT, tile, 0)
    lax.fori_loop(0, NT - 4, svcc, 0)
    svcb(jnp.int32(NT - 1))
    lax.fori_loop(NT - 4, NT, svcc, 0)

    for i in range(1, ng):
        d = lax.rem(me + i, ng)
        rc(gsend.at[d], grecv.at[me], g_ssem.at[i], g_rsem.at[i], d).wait_send()

    def drain_ag(c, _):
        for typ, rows in ((0, lo), (1, hi), (2, hi), (3, lo), (4, lo), (5, hi), (6, None), (7, None), (8, None), (9, None)):
            ag(c, typ, sib, me, rows).wait_send()
        return 0

    lax.fori_loop(0, NC, drain_ag, 0)

    def drain_rs(ct, _):
        @pl.when(ct >= NT - 2)
        def _():
            dcopy(ct, lax.rem(ct, 2), sib).wait_send()
        for i in range(2):
            hcopy(ct, i).wait_send()
            fcopy(ct, i).wait_send()
        return 0

    lax.fori_loop(0, NT, drain_rs, 0)


def solution(mesh):
    ng = mesh.shape["ep"]
    nq = ng // 2

    def moe_step(tokens, expert_ids, gate_vals, w_gate, w_up, w_down, shared_gate, shared_up, shared_down):
        T, D = tokens.shape
        top = expert_ids.shape[1]
        E, _, F = w_gate.shape
        SF = shared_gate.shape[1]
        spread = max(ng, E * ng // 2)
        cap = (T * top + spread - 1) // spread
        W = D // NC
        TC = W // 2
        NT = D // TC
        R = 2 * cap
        M = nq * R
        dims = (ng, nq, T, D, F, SF, E, cap, top)
        any_spec = pl.BlockSpec(memory_space=pl.ANY)
        vm_spec = pl.BlockSpec(memory_space=pltpu.VMEM)
        dma = pltpu.SemaphoreType.DMA
        flops = 2 * 3 * D * (E * M * F + T * SF)
        return pl.pallas_call(
            functools.partial(moe_kernel, dims),
            out_shape=jax.ShapeDtypeStruct((T, D), BF16),
            in_specs=[vm_spec, vm_spec] + [any_spec] * 7,
            out_specs=vm_spec,
            scratch_shapes=[
                pltpu.VMEM((NC, ng, T, W), BF16),
                pltpu.VMEM((T, D), BF16),
                pltpu.VMEM((E, M, W), BF16),
                pltpu.VMEM((E, M, 2 * F), F32),
                pltpu.VMEM((E, M, F), BF16),
                pltpu.VMEM((nq, E, R, TC), BF16),
                pltpu.VMEM((2, 2, nq, T, TC), F32),
                pltpu.VMEM((NT, nq, T, TC), F32),
                pltpu.VMEM((NT, 2, T // 2, TC), F32),
                pltpu.VMEM((NT, 2, T, TC), F32),
                pltpu.VMEM((nq, E, R, 2 * T), BF16),
                pltpu.VMEM((nq, 3, 2 * T, E * R), BF16),
                pltpu.VMEM((T, SF), BF16),
                pltpu.VMEM((T, W), F32),
                pltpu.VMEM((T, D), BF16),
                pltpu.VMEM((ng, E, T), F32),
                pltpu.VMEM((ng, E, T), F32),
                pltpu.VMEM((ng, E, T), F32),
                pltpu.VMEM((NS, SF, W), BF16),
                dma((NS,)), dma((NC + 1,)), dma((ng,)), dma((ng,)),
                dma((NC, 10)), dma((NC, 10)), dma((NT,)), dma((NT,)),
                dma((NT, 2)), dma((NT, 2)), dma((NT, 2)), dma((NT, 2)),
            ],
            compiler_params=pltpu.CompilerParams(collective_id=0, has_side_effects=True, vmem_limit_bytes=67043328),
            cost_estimate=pl.CostEstimate(flops=flops, bytes_accessed=2 * 3 * D * (E * F + SF), transcendentals=0),
        )(expert_ids.T, gate_vals.T, tokens, w_gate, w_up, w_down, shared_gate, shared_up, shared_down)

    row_spec = P(("dp", "ep"), None)
    expert_spec = P("ep", None, None)
    whole_spec = P(None, None)
    return jax.shard_map(moe_step, mesh=mesh, in_specs=(row_spec, row_spec, row_spec, expert_spec, expert_spec, expert_spec, whole_spec, whole_spec, whole_spec), out_specs=row_spec, check_vma=False)
```

time: 327 us -> 125 us (0.38)
  Pallas kernels: 0 us -> 123 us
  matrix products: 105 us -> 0 us
  blocking collectives: 93.8 us -> 0 us
  waiting for transfers between devices: 79.1 us -> 0 us
  local copies, waits for them, and re-layouts: 30.1 us -> 1.97 us
  other arithmetic: 12.1 us -> 0 us
  starting transfers between devices: 6.04 us -> 0 us
    pallas_call x0 -> x1, Pallas kernels: none -> 123 us  [moe_step(): pl.pallas_call(functools.partial(moe_kernel, dims), out_shape=jax.ShapeDt...]
    dot_general x5 -> x0, matrix products: 105 us -> none  [the longest x1 51.1 us: expert_block(): jnp.einsum('slcf,lfd->slcd', hidden, w_down, preferred_element_type=jnp.f...]
    all_to_all x1 -> x0, blocking collectives: 93.8 us -> none  [moe_step(): recv_buf = lax.all_to_all(send_buf, 'ep', 0, 0, tiled=True)]
    all_to_all x1 -> x0, waiting for transfers between devices: 79.1 us -> none  [moe_step(): lax.all_to_all(expert_out.reshape(expert_count * capacity, model_dim), 'e...]
    gather x2 -> x0, local copies, waits for them, and re-layouts: 19.7 us -> none  [moe_step(): picked = jnp.take(back_buf, columns, axis=0)]
    reduce_sum x2 -> x0, other arithmetic: 8.24 us -> none  [the longest x1 8.11 us: moe_step(): jnp.sum(gate_vals[:, :, None] * picked.astype(jnp.float32), axis=1)]
    convert_element_type x1 -> x0, local copies, waits for them, and re-layouts: 7.06 us -> none  [expert_block(): jnp.einsum('slcf,lfd->slcd', hidden, w_down, preferred_element_type=jnp.f...]
    all_to_all x1 -> x0, starting transfers between devices: 6.04 us -> none  [moe_step(): lax.all_to_all(expert_out.reshape(expert_count * capacity, model_dim), 'e...]
  transfers between devices with their start and end apart: 1 -> 0, of which waited for: 1 -> 0; matrix products, arithmetic and copies ran while one was open for 3% -> 0% of each run, Pallas kernels for 0% -> 0%
where the time goes in v1:
time: 125 us
  Pallas kernels  123 us (98%)
  local copies, waits for them, and re-layouts  1.97 us (2%)
    pallas_call x1, Pallas kernels, moe_step(): pl.pallas_call(functools.partial(moe_kernel, dims), out_shape=jax.ShapeDt...  123 us

profile of v1, /device:TPU:81, one launch (start us, length us, event | category | flops | bytes accessed | tf_op | source)
XLA Modules:
  0.0 124.7 jit_solution(1844160392654417719)
XLA Ops:
  0.0 122.8 %shard_map.91 = bf16[128,2560]{1,0:T(8,128)(2,1)} custom-call(s32[6,128]{1,0:T(8,128)} %bitcast.2, f32[6,128]{1,0:T(8,128)} %bitcast.3, bf16[128,2560]{1,0:T(8,128)(2,1)} %tok.1, bf16[8,2560,1536]{2,1,0:T(8,128)(2,1)} %wg.1, bf16[8,2560,1536]{2,1,0:T(8,128)(2,1)} %wu.1, bf16[8,1536,2560]{2,1,0:T(8,128)(2,1)} %wd.1, bf16[2560,3072]{1,0:T(8,128)(2,1)} %sg.1, ...), custom_call_target="tpu_custom_call" | custom-call | flops 42278584320 | bytes 235929600 | tf_op jit(solution)/shard_map/pallas_call | solution.py:402
  122.8 2.0 %copy.11 = bf16[128,2560]{1,0:T(8,128)(2,1)} copy(bf16[128,2560]{1,0:T(8,128)(2,1)} %shard_map.91) | data formatting | bytes 1310720

commit v2 on v1

--- a/solution.py
+++ b/solution.py
@@ -11,11 +11,12 @@
 BF16 = jnp.bfloat16
 NS = 5
 NC = 5
+KS = 8
 
 
 def moe_kernel(dims, ids_ref, gates_ref, tok, wg, wu, wd, sg, su, sd, out_ref,
-               xall, xown, xg, acc, h, y, pst, dsum, hrecv, frecv, oh, gt, hs, sgacc, shr, posr, grecv, gsend, slots,
-               slot_sem, loc_sem, g_ssem, g_rsem, a_ssem, a_rsem, d_ssem, d_rsem, h_ssem, h_rsem, f_ssem, f_rsem):
+               xall, xown, xg, acc, h, y, pst, dsum, rmsg, oh, gt, hs, sgacc, shr, posr, grecv, gsend, slots,
+               slot_sem, loc_sem, g_ssem, g_rsem, a_ssem, a_rsem, d_ssem, d_rsem, m_ssem, m_rsem):
     ng, nq, T, D, F, SF, E, cap, top = dims
     W = D // NC
     TC = W // 2
@@ -25,8 +26,11 @@
     HT = T // 2
     FJ = F // W
     SFJ = SF // W
-    n1 = NC * E
-    ntot = n1 + 2 * NT + 2 * SFJ + NC
+    n1 = KS + NC * E
+    ns = 2 * SFJ + NC
+    ntot = KS + NC * E + 2 * NT + ns - KS
+    nm = NT + 2
+    MR = HT + T
 
     me = lax.axis_index("ep")
     q = me // 2
@@ -47,10 +51,10 @@
         sl = lax.rem(n, NS)
         sem = slot_sem.at[sl]
 
-        @pl.when(n < n1)
-        def _():
-            c = n // E
-            e = lax.rem(n, E)
+        @pl.when((n >= KS) & (n < n1))
+        def _():
+            c = (n - KS) // E
+            e = lax.rem(n - KS, E)
             for j in range(FJ):
                 pltpu.make_async_copy(wg.at[e, pl.ds(pl.multiple_of(c * W, W), W), pl.ds(j * W, W)],
                                       slots.at[sl, pl.ds(j * W, W), :], sem).start()
@@ -58,20 +62,18 @@
                 pltpu.make_async_copy(wu.at[e, pl.ds(pl.multiple_of(c * W, W), W), pl.ds(j * W, W)],
                                       slots.at[sl, pl.ds((FJ + j) * W, W), :], sem).start()
 
-        m = n - n1
-        last = n >= ntot - 2
-        r = lax.rem(m, 4)
-        ct = jnp.where(last, NT - 1, m // 4)
-        half = jnp.where(last, n - (ntot - 2), r)
-
-        @pl.when((n >= n1) & (n < ntot) & ((r < 2) | last))
+        m = jnp.maximum(n - n1, 0)
+        ct = m // 3
+        half = lax.rem(m, 3)
+
+        @pl.when((n >= n1) & (n < ntot) & (half < 2))
         def _():
             for j in range(E // 2):
                 pltpu.make_async_copy(wd.at[half * (E // 2) + j, :, pl.ds(pl.multiple_of(ct * TC, TC), TC)],
                                       slots.at[sl, pl.ds((j // 2) * F, F), pl.ds((j % 2) * TC, TC)], sem).start()
 
-        s = 2 * (m // 4) + r - 2
-        shared = (n >= n1) & (n < ntot - 2) & (r >= 2)
+        s = jnp.where(n < KS, n, KS + ct)
+        shared = (n < KS) | ((n >= n1) & (n < ntot) & (half == 2))
         fcol = pl.ds(pl.multiple_of((s // 2) * W, W), W)
 
         @pl.when(shared & (s < 2 * SFJ) & (lax.rem(s, 2) == 0))
@@ -130,10 +132,6 @@
         ag(c, 2, right, right, hi).wait_recv()
         ag(c, 5, left, right, hi).start()
 
-        @pl.when(c + 1 < NC)
-        def _():
-            own(c + 1)
-
     def svc1(c):
         ag(c, 1, left, left, hi).wait_recv()
         ag(c, 7, sib, left, None).start()
@@ -152,6 +150,44 @@
         ag(c, 8, sib, sr_, None).wait_recv()
         ag(c, 9, sib, so_, None).wait_recv()
 
+    def shared_gu(s, n):
+        sl = lax.rem(n, NS)
+        fcol = pl.ds(pl.multiple_of((s // 2) * W, W), W)
+
+        @pl.when(lax.rem(s, 2) == 0)
+        def _():
+            wait_gu(sl)
+            sgacc[...] = jnp.dot(xown[...], slots[sl, :D, :], preferred_element_type=F32)
+
+        @pl.when(lax.rem(s, 2) == 1)
+        def _():
+            wait_gu(sl)
+            uv = jnp.dot(xown[...], slots[sl, :D, :], preferred_element_type=F32)
+            gv = sgacc[...]
+            hs[:, fcol] = (gv * jax.nn.sigmoid(gv) * uv).astype(BF16)
+
+    def shared_step(s, n):
+        sl = lax.rem(n, NS)
+
+        @pl.when(s < 2 * SFJ)
+        def _():
+            shared_gu(s, n)
+
+        @pl.when(s >= 2 * SFJ)
+        def _():
+            wait_full(sl)
+            col = pl.ds(pl.multiple_of((s - 2 * SFJ) * W, W), W)
+            shr[:, col] = jnp.dot(hs[...], slots[sl], preferred_element_type=F32).astype(BF16)
+
+        issue(n + NS)
+
+    def early(first, last):
+        def body(n, _):
+            shared_gu(n, n)
+            issue(n + NS)
+            return 0
+        lax.fori_loop(first, last, body, 0)
+
     for c in range(NC):
         xcopies[c].wait()
     own(jnp.int32(0))
@@ -159,10 +195,14 @@
         d = lax.rem(me + i, ng)
         rc(gsend.at[d], grecv.at[me], g_ssem.at[i], g_rsem.at[i], d).start()
 
+    xcopies[NC].wait()
+    early(0, 3)
     for e in range(E):
         acc[e] = jnp.zeros((M, 2 * F), F32)
-
+    early(3, 4)
     svc0(jnp.int32(0))
+    early(4, 5)
+    svc1(jnp.int32(0))
 
     for i in range(1, ng):
         s = lax.rem(me + ng - i, ng)
@@ -174,31 +214,30 @@
     pos = jnp.dot(mask.astype(F32).astype(BF16), tri, preferred_element_type=F32)
     posr[...] = jnp.where(mask, pos, -1000.0).reshape(ng, E, T)
 
-    svc1(jnp.int32(0))
-
     riota = lax.broadcasted_iota(jnp.int32, (R, T), 0).astype(F32)
+    ciota = lax.broadcasted_iota(jnp.int32, (cap, T), 0).astype(F32)
 
     def route(b, _):
-        parts = []
         for e in range(E):
-            hits, gs = [], []
-            for s in range(2):
-                hit = posr[2 * b + s, e:e + 1, :] == (riota - float(s * cap))
-                hits.append(jnp.where(hit, 1.0, 0.0))
-                gs.append(jnp.where(hit, grecv[2 * b + s, e:e + 1, :], 0.0))
+            hits = [jnp.where(posr[2 * b + s, e:e + 1, :] == (riota - float(s * cap)), 1.0, 0.0) for s in range(2)]
             oh[b, e] = jnp.concatenate(hits, axis=1).astype(BF16)
-            parts.append(jnp.concatenate(gs, axis=1))
-        g = jnp.concatenate(parts, axis=0).T
-        g0 = g.astype(BF16)
-        rem = g - g0.astype(F32)
-        g1 = rem.astype(BF16)
-        gt[b, 0] = g0
-        gt[b, 1] = g1
-        gt[b, 2] = (rem - g1.astype(F32)).astype(BF16)
+        for s in range(2):
+            src = 2 * b + s
+            g = jnp.concatenate([jnp.where(posr[src, e:e + 1, :] == ciota, grecv[src, e:e + 1, :], 0.0)
+                                 for e in range(E)], axis=0).T
+            g0 = g.astype(BF16)
+            rem = g - g0.astype(F32)
+            g1 = rem.astype(BF16)
+            gt[src, :T] = g0
+            gt[src, T:2 * T] = g1
+            gt[src, 2 * T:] = (rem - g1.astype(F32)).astype(BF16)
         return 0
 
     lax.fori_loop(0, nq, route, 0)
+    early(5, 6)
     svc2(jnp.int32(0))
+    own(jnp.int32(1))
+    early(6, KS)
 
     def chunk(c, _):
         need(c)
@@ -209,7 +248,7 @@
             xg[:, b * R:(b + 1) * R, :] = rows.reshape(E, R, W)
 
         def estep(e, _):
-            n = c * E + e
+            n = KS + c * E + e
             sl = lax.rem(n, NS)
             wait_full(sl)
             xe = xg[e]
@@ -224,15 +263,21 @@
                     uv = acc[e, :, F + j * W:F + (j + 1) * W]
                     h[e, :, j * W:(j + 1) * W] = (gv * jax.nn.sigmoid(gv) * uv).astype(BF16)
 
-            @pl.when((c < NC - 1) & (e == 1))
+            lag = jnp.where(c == 0, 3, 0)
+
+            @pl.when((c < NC - 1) & (e == lag))
             def _():
                 svc0(c + 1)
 
-            @pl.when((c < NC - 1) & (e == 3))
+            @pl.when((c < NC - 1) & (e == lag + 1))
             def _():
                 svc1(c + 1)
 
-            @pl.when((c < NC - 1) & (e == E - 2))
+                @pl.when(c < NC - 2)
+                def _():
+                    own(c + 2)
+
+            @pl.when((c < NC - 1) & (e == lag + 4))
             def _():
                 svc2(c + 1)
             return 0
@@ -245,115 +290,111 @@
     def dcopy(ct, buf, dev):
         return rc(pst.at[buf, 1 - k], dsum.at[ct], d_ssem.at[ct], d_rsem.at[ct], dev)
 
-    def hcopy(ct, i):
-        rows = (lo, hi)[i]
-        return rc(dsum.at[ct, oq, rows, :], hrecv.at[ct, i], h_ssem.at[ct, i], h_rsem.at[ct, i], (right, left)[i])
-
-    def fcopy(ct, i):
-        return rc(dsum.at[ct, (rq, lq)[i]], frecv.at[ct, i], f_ssem.at[ct, i], f_rsem.at[ct, i], (right, left)[i])
-
-    def svca(ct):
-        dcopy(ct, lax.rem(ct, 2), sib).wait_recv()
-        for d in (oq, rq, lq, q):
-            dsum[ct, d] += pst[lax.rem(ct, 2), k, d]
-        hcopy(ct, 0).start()
-        hcopy(ct, 1).start()
-
-    def svcb(ct):
-        hcopy(ct, 0).wait_recv()
-        dsum[ct, rq, :HT, :] += hrecv[ct, 0]
-        fcopy(ct, 0).start()
-        hcopy(ct, 1).wait_recv()
-        dsum[ct, lq, HT:, :] += hrecv[ct, 1]
-        fcopy(ct, 1).start()
+    spans = (pl.ds(0, HT), pl.ds(0, MR), pl.ds(HT, T))
+
+    def mblock(g, i):
+        x = 2 * g + i
+        per = 2 * F // TC
+        return x // per, pl.ds(pl.multiple_of(lax.rem(x, per) * TC, TC), TC)
+
+    def mcopy(g, i, kind):
+        e, cols = mblock(g, i)
+        return rc(acc.at[e, spans[kind], cols], rmsg.at[g, i, spans[kind], :], m_ssem.at[g, i], m_rsem.at[g, i],
+                  (right, left)[i])
+
+    def mdo(g, what):
+        for kind, cond in ((0, g < 2), (1, (g >= 2) & (g < NT)), (2, g >= NT)):
+            @pl.when(cond)
+            def _():
+                for i in range(2):
+                    getattr(mcopy(g, i, kind), what)()
+
+    def svcm_new(ct):
+        buf = lax.rem(ct, 2)
+        dcopy(ct, buf, sib).wait_recv()
+        for i, rows in ((0, lo), (1, hi)):
+            e, cols = mblock(ct, i)
+            acc[e, :HT, cols] = dsum[ct, oq, rows, :] + pst[buf, k, oq, rows, :]
+        for d in (rq, lq, q):
+            dsum[ct, d] += pst[buf, k, d]
+
+    def svcm_old(ct):
+        g = ct - 2
+        mdo(g, "wait_recv")
+        e, cols = mblock(ct, 0)
+        acc[e, HT:2 * HT, cols] = dsum[g, rq, :HT, :] + rmsg[g, 0, :HT, :]
+        acc[e, 2 * HT:MR, cols] = dsum[g, rq, HT:, :]
+        e, cols = mblock(ct, 1)
+        acc[e, HT:2 * HT, cols] = dsum[g, lq, :HT, :]
+        acc[e, 2 * HT:MR, cols] = dsum[g, lq, HT:, :] + rmsg[g, 1, :HT, :]
+
+    def message(ct):
+        svcm_new(ct)
+
+        @pl.when(ct >= 2)
+        def _():
+            svcm_old(ct)
+
+        mdo(ct, "start")
 
     def svcc(ct, _):
-        fcopy(ct, 0).wait_recv()
-        fcopy(ct, 1).wait_recv()
         cols = pl.ds(pl.multiple_of(ct * TC, TC), TC)
-        routed = dsum[ct, q] + frecv[ct, 0] + frecv[ct, 1]
+        routed = dsum[ct, q] + rmsg[ct + 2, 0, HT:, :] + rmsg[ct + 2, 1, HT:, :]
         out_ref[:, cols] = (xown[:, cols].astype(F32) + routed + shr[:, cols].astype(F32)).astype(BF16)
         return 0
-
-    def shared_step(s, n):
-        sl = lax.rem(n, NS)
-        fcol = pl.ds(pl.multiple_of((s // 2) * W, W), W)
-
-        @pl.when((s < 2 * SFJ) & (lax.rem(s, 2) == 0))
-        def _():
-            wait_gu(sl)
-            sgacc[...] = jnp.dot(xown[...], slots[sl, :D, :], preferred_element_type=F32)
-
-        @pl.when((s < 2 * SFJ) & (lax.rem(s, 2) == 1))
-        def _():
-            wait_gu(sl)
-            uv = jnp.dot(xown[...], slots[sl, :D, :], preferred_element_type=F32)
-            gv = sgacc[...]
-            hs[:, fcol] = (gv * jax.nn.sigmoid(gv) * uv).astype(BF16)
-
-        @pl.when(s >= 2 * SFJ)
-        def _():
-            wait_full(sl)
-            col = pl.ds(pl.multiple_of((s - 2 * SFJ) * W, W), W)
-            shr[:, col] = jnp.dot(hs[...], slots[sl], preferred_element_type=F32).astype(BF16)
-
-        issue(n + NS)
-
-    xcopies[NC].wait()
 
     def tile(ct, _):
         buf = lax.rem(ct, 2)
-        base = n1 + 4 * ct - jnp.where(ct == NT - 1, 1, 0)
-
-        def dstep(half, _):
+        base = n1 + 3 * ct
+
+        def dstep(half):
             n = base + half
             sl = lax.rem(n, NS)
             wait_full(sl)
-            for j in range(E // 2):
-                e = half * (E // 2) + j
-                w = slots[sl, (j // 2) * F:(j // 2 + 1) * F, (j % 2) * TC:(j % 2 + 1) * TC]
-                ye = jnp.dot(h[e], w, preferred_element_type=F32).astype(BF16)
-                y[:, e] = ye.reshape(nq, R, TC)
+            for p in range(E // 4):
+                ys = []
+                for j in (2 * p, 2 * p + 1):
+                    w = slots[sl, (j // 2) * F:(j // 2 + 1) * F, (j % 2) * TC:(j % 2 + 1) * TC]
+                    ye = jnp.dot(h[half * (E // 2) + j], w, preferred_element_type=F32)
+                    ys.append(ye.reshape(ng, cap, TC))
+                y[:, half * (E // 4) + p] = jnp.concatenate(ys, axis=1).astype(BF16)
             issue(n + NS)
-            return 0
-
-        lax.fori_loop(0, 2, dstep, 0)
+
+        dstep(0)
+        dstep(1)
 
         @pl.when(ct >= 2)
         def _():
             dcopy(ct - 2, buf, sib).wait_send()
 
         def combine(b, _):
-            yb = y[b].reshape(E * R, TC)
-            p = jnp.dot(gt[b, 0], yb, preferred_element_type=F32)
-            p = p + jnp.dot(gt[b, 1], yb, preferred_element_type=F32)
-            p = p + jnp.dot(gt[b, 2], yb, preferred_element_type=F32)
-            pst[buf, 0, b] = p[:T]
-            pst[buf, 1, b] = p[T:]
+            for core in range(2):
+                src = 2 * b + core
+                p = jnp.dot(gt[src], y[src].reshape(E * cap, TC), preferred_element_type=F32)
+                pst[buf, core, b] = p[:T] + p[T:2 * T] + p[2 * T:]
             return 0
 
         lax.fori_loop(0, nq, combine, 0)
         dcopy(ct, buf, sib).start()
 
-        @pl.when(ct < NT - 1)
-        def _():
-            shared_step(2 * ct, base + 2)
-
-        svca(ct)
+        @pl.when(KS + ct < ns)
+        def _():
+            shared_step(KS + ct, base + 2)
 
         @pl.when(ct >= 1)
         def _():
-            svcb(ct - 1)
-
-        @pl.when(ct < NT - 2)
-        def _():
-            shared_step(2 * ct + 1, base + 3)
+            message(ct - 1)
         return 0
 
     lax.fori_loop(0, NT, tile, 0)
-    lax.fori_loop(0, NT - 4, svcc, 0)
-    svcb(jnp.int32(NT - 1))
-    lax.fori_loop(NT - 4, NT, svcc, 0)
+    message(jnp.int32(NT - 1))
+    for g in (NT, NT + 1):
+        svcm_old(jnp.int32(g))
+        mdo(jnp.int32(g), "start")
+    lax.fori_loop(0, NT - 2, svcc, 0)
+    for g in (NT, NT + 1):
+        mdo(jnp.int32(g), "wait_recv")
+        svcc(jnp.int32(g - 2), 0)
 
     for i in range(1, ng):
         d = lax.rem(me + i, ng)
@@ -367,15 +408,13 @@
     lax.fori_loop(0, NC, drain_ag, 0)
 
     def drain_rs(ct, _):
-        @pl.when(ct >= NT - 2)
+        @pl.when((ct >= NT - 2) & (ct < NT))
         def _():
             dcopy(ct, lax.rem(ct, 2), sib).wait_send()
-        for i in range(2):
-            hcopy(ct, i).wait_send()
-            fcopy(ct, i).wait_send()
-        return 0
-
-    lax.fori_loop(0, NT, drain_rs, 0)
+        mdo(ct, "wait_send")
+        return 0
+
+    lax.fori_loop(0, nm, drain_rs, 0)
 
 
 def solution(mesh):
@@ -410,13 +449,12 @@
                 pltpu.VMEM((E, M, W), BF16),
                 pltpu.VMEM((E, M, 2 * F), F32),
                 pltpu.VMEM((E, M, F), BF16),
-                pltpu.VMEM((nq, E, R, TC), BF16),
+                pltpu.VMEM((ng, E // 2, R, TC), BF16),
                 pltpu.VMEM((2, 2, nq, T, TC), F32),
                 pltpu.VMEM((NT, nq, T, TC), F32),
-                pltpu.VMEM((NT, 2, T // 2, TC), F32),
-                pltpu.VMEM((NT, 2, T, TC), F32),
+                pltpu.VMEM((NT + 2, 2, T + T // 2, TC), F32),
                 pltpu.VMEM((nq, E, R, 2 * T), BF16),
-                pltpu.VMEM((nq, 3, 2 * T, E * R), BF16),
+                pltpu.VMEM((ng, 3 * T, E * cap), BF16),
                 pltpu.VMEM((T, SF), BF16),
                 pltpu.VMEM((T, W), F32),
                 pltpu.VMEM((T, D), BF16),
@@ -426,7 +464,7 @@
                 pltpu.VMEM((NS, SF, W), BF16),
                 dma((NS,)), dma((NC + 1,)), dma((ng,)), dma((ng,)),
                 dma((NC, 10)), dma((NC, 10)), dma((NT,)), dma((NT,)),
-                dma((NT, 2)), dma((NT, 2)), dma((NT, 2)), dma((NT, 2)),
+                dma((NT + 2, 2)), dma((NT + 2, 2)),
             ],
             compiler_params=pltpu.CompilerParams(collective_id=0, has_side_effects=True, vmem_limit_bytes=67043328),
             cost_estimate=pl.CostEstimate(flops=flops, bytes_accessed=2 * 3 * D * (E * F + SF), transcendentals=0),

time: 125 us -> 117 us (0.936)
  Pallas kernels: 123 us -> 115 us
    pallas_call x1, Pallas kernels: 123 us -> 115 us  [moe_step(): pl.pallas_call(functools.partial(moe_kernel, dims), out_shape=jax.ShapeDt...]
where the time goes in v2:
time: 117 us
  Pallas kernels  115 us (98%)
  local copies, waits for them, and re-layouts  1.97 us (2%)
    pallas_call x1, Pallas kernels, moe_step(): pl.pallas_call(functools.partial(moe_kernel, dims), out_shape=jax.ShapeDt...  115 us

profile of v2, /device:TPU:81, one launch (start us, length us, event | category | flops | bytes accessed | tf_op | source)
XLA Modules:
  0.0 117.0 jit_solution(14778997248275301842)
XLA Ops:
  0.0 115.0 %shard_map.91 = bf16[128,2560]{1,0:T(8,128)(2,1)} custom-call(s32[6,128]{1,0:T(8,128)} %bitcast.2, f32[6,128]{1,0:T(8,128)} %bitcast.3, bf16[128,2560]{1,0:T(8,128)(2,1)} %tok.1, bf16[8,2560,1536]{2,1,0:T(8,128)(2,1)} %wg.1, bf16[8,2560,1536]{2,1,0:T(8,128)(2,1)} %wu.1, bf16[8,1536,2560]{2,1,0:T(8,128)(2,1)} %wd.1, bf16[2560,3072]{1,0:T(8,128)(2,1)} %sg.1, ...), custom_call_target="tpu_custom_call" | custom-call | flops 42278584320 | bytes 235929600 | tf_op jit(solution)/shard_map/pallas_call | solution.py:441
  115.0 2.0 %copy.11 = bf16[128,2560]{1,0:T(8,128)(2,1)} copy(bf16[128,2560]{1,0:T(8,128)(2,1)} %shard_map.91) | data formatting | bytes 1310720

commit v3 on v2

--- a/solution.py
+++ b/solution.py
@@ -28,7 +28,8 @@
     SFJ = SF // W
     n1 = KS + NC * E
     ns = 2 * SFJ + NC
-    ntot = KS + NC * E + 2 * NT + ns - KS
+    n2 = n1 + 2 * NT
+    ntot = n2 + ns - KS
     nm = NT + 2
     MR = HT + T
 
@@ -63,17 +64,17 @@
                                       slots.at[sl, pl.ds((FJ + j) * W, W), :], sem).start()
 
         m = jnp.maximum(n - n1, 0)
-        ct = m // 3
-        half = lax.rem(m, 3)
-
-        @pl.when((n >= n1) & (n < ntot) & (half < 2))
+        ct = m // 2
+        half = lax.rem(m, 2)
+
+        @pl.when((n >= n1) & (n < n2))
         def _():
             for j in range(E // 2):
                 pltpu.make_async_copy(wd.at[half * (E // 2) + j, :, pl.ds(pl.multiple_of(ct * TC, TC), TC)],
                                       slots.at[sl, pl.ds((j // 2) * F, F), pl.ds((j % 2) * TC, TC)], sem).start()
 
-        s = jnp.where(n < KS, n, KS + ct)
-        shared = (n < KS) | ((n >= n1) & (n < ntot) & (half == 2))
+        s = jnp.where(n < KS, n, n - n2 + KS)
+        shared = (n < KS) | ((n >= n2) & (n < ntot))
         fcol = pl.ds(pl.multiple_of((s // 2) * W, W), W)
 
         @pl.when(shared & (s < 2 * SFJ) & (lax.rem(s, 2) == 0))
@@ -345,7 +346,7 @@
 
     def tile(ct, _):
         buf = lax.rem(ct, 2)
-        base = n1 + 3 * ct
+        base = n1 + 2 * ct
 
         def dstep(half):
             n = base + half
@@ -377,10 +378,6 @@
         lax.fori_loop(0, nq, combine, 0)
         dcopy(ct, buf, sib).start()
 
-        @pl.when(KS + ct < ns)
-        def _():
-            shared_step(KS + ct, base + 2)
-
         @pl.when(ct >= 1)
         def _():
             message(ct - 1)
@@ -388,9 +385,18 @@
 
     lax.fori_loop(0, NT, tile, 0)
     message(jnp.int32(NT - 1))
-    for g in (NT, NT + 1):
-        svcm_old(jnp.int32(g))
-        mdo(jnp.int32(g), "start")
+
+    def tail(i, _):
+        shared_step(KS + i, n2 + i)
+
+        @pl.when((i == 2) | (i == 5))
+        def _():
+            g = NT + i // 3
+            svcm_old(g)
+            mdo(g, "start")
+        return 0
+
+    lax.fori_loop(0, ns - KS, tail, 0)
     lax.fori_loop(0, NT - 2, svcc, 0)
     for g in (NT, NT + 1):
         mdo(jnp.int32(g), "wait_recv")

time: 117 us -> 115 us (0.983)
  Pallas kernels: 115 us -> 113 us
    pallas_call x1, Pallas kernels: 115 us -> 113 us  [moe_step(): pl.pallas_call(functools.partial(moe_kernel, dims), out_shape=jax.ShapeDt...]
where the time goes in v3:
time: 115 us
  Pallas kernels  113 us (98%)
  local copies, waits for them, and re-layouts  1.97 us (2%)
    pallas_call x1, Pallas kernels, moe_step(): pl.pallas_call(functools.partial(moe_kernel, dims), out_shape=jax.ShapeDt...  113 us

profile of v3, /device:TPU:81, one launch (start us, length us, event | category | flops | bytes accessed | tf_op | source)
XLA Modules:
  0.0 114.6 jit_solution(4808810545305114119)
XLA Ops:
  0.0 112.6 %shard_map.91 = bf16[128,2560]{1,0:T(8,128)(2,1)} custom-call(s32[6,128]{1,0:T(8,128)} %bitcast.2, f32[6,128]{1,0:T(8,128)} %bitcast.3, bf16[128,2560]{1,0:T(8,128)(2,1)} %tok.1, bf16[8,2560,1536]{2,1,0:T(8,128)(2,1)} %wg.1, bf16[8,2560,1536]{2,1,0:T(8,128)(2,1)} %wu.1, bf16[8,1536,2560]{2,1,0:T(8,128)(2,1)} %wd.1, bf16[2560,3072]{1,0:T(8,128)(2,1)} %sg.1, ...), custom_call_target="tpu_custom_call" | custom-call | flops 42278584320 | bytes 235929600 | tf_op jit(solution)/shard_map/pallas_call | solution.py:447
  112.6 2.0 %copy.11 = bf16[128,2560]{1,0:T(8,128)(2,1)} copy(bf16[128,2560]{1,0:T(8,128)(2,1)} %shard_map.91) | data formatting | bytes 1310720
